TPU v7x, 32 devices: a whole 2x2x4 slice. The times are simulated.
32 devices in a mesh: ctx: 2 (over core), head: 4 (over y, x), doc: 4 (over z).
Axes of the slice: x: 2, y: 2, z: 4, core: 2. Of those that a mesh axis runs over, the one named last changes fastest.
Arguments:
- queries: bfloat16 [4, 256, 8192], P('doc', 'ctx', 'head'), may hold values from -360 to 360
- keys: bfloat16 [4, 8192, 1024], P('doc', 'ctx', 'head'), may hold values from -6 to 6
- values: bfloat16 [4, 8192, 1024], P('doc', 'ctx', 'head'), may hold values from -6 to 6
- pattern: int32 [4, 2, 16], P('doc'), may hold values from 0 to 63, as said below
Outputs:
- attended: bfloat16 [4, 256, 8192], P('doc', 'ctx', 'head')
- gram: float32 [8192, 8192], P(('head', 'ctx'), 'doc')
Inputs may be any that keep to these rules, and one draw needn't show every extreme that they name: Each row pattern[d, b, :] lists 16 different block numbers; no context shard (blocks s * 32 to (s + 1) * 32 - 1) holds more than 12 of one row's blocks, and in every draw some row has exactly 12 of its blocks in one shard.
All inputs are finite; a program needn't handle non-finite values.
Results may differ from a plain program's by a relative error of at most 0.015.
Values may be sent and summed in bfloat16 or wider, within the bound.
A program may use at most 128 MiB of HBM per device.

v0:
```python
import jax
import jax.numpy as jnp
from jax import lax
from jax.sharding import PartitionSpec as P

HEAD_SIZE = 128
BLOCK_TOKENS = 128
QB_DEV = 1
NKB_DEV = 32
GROUP = 8
CAP = 12


NEGATIVE = -1e30


def joined(value, axis, join):
    pieces = jax.tree.map(lambda part: lax.all_gather(part, axis), value)
    head = jax.tree.map(lambda part: part[0], pieces)
    tail = jax.tree.map(lambda part: part[1:], pieces)
    so_far, _ = lax.scan(lambda so_far, share: (join(so_far, share), None), head, tail)
    return so_far


def owned_slots(pattern_rows, owner):
    mine = pattern_rows // NKB_DEV == owner
    order = jnp.argsort(1 - mine.astype(jnp.int32), axis=1, stable=True)[:, :CAP]
    picked = jnp.take_along_axis(pattern_rows, order, axis=1) % NKB_DEV
    valid = jnp.take_along_axis(mine, order, axis=1)
    return (picked, valid)


def attend_block(query, key_blocks, value_blocks, valid):
    slots = key_blocks.shape[0]
    kv_heads = key_blocks.shape[2] // HEAD_SIZE
    grouped = query.reshape(BLOCK_TOKENS, kv_heads, GROUP, HEAD_SIZE)
    key_row_list = key_blocks.reshape(slots * BLOCK_TOKENS, kv_heads, HEAD_SIZE)
    value_row_list = value_blocks.reshape(slots * BLOCK_TOKENS, kv_heads, HEAD_SIZE)
    scores = jnp.einsum(
        "qkgd,skd->kgqs", grouped, key_row_list, preferred_element_type=jnp.float32
    ) * HEAD_SIZE ** (-0.5)
    live = jnp.broadcast_to(valid[:, None], (slots, BLOCK_TOKENS)).reshape(slots * BLOCK_TOKENS)
    scores = jnp.where(live, scores, NEGATIVE)
    top = jnp.max(scores, axis=-1)
    weights = jnp.where(live, jnp.exp(scores - top[..., None]), 0.0)
    total = jnp.sum(weights, axis=-1)
    mixed = jnp.einsum(
        "kgqs,skd->qkgd",
        weights.astype(jnp.bfloat16),
        value_row_list,
        preferred_element_type=jnp.float32,
    )
    heads = kv_heads * GROUP
    top_rows = jnp.transpose(top, (2, 0, 1)).reshape(BLOCK_TOKENS, heads)
    total_rows = jnp.transpose(total, (2, 0, 1)).reshape(BLOCK_TOKENS, heads)
    return (mixed.reshape(BLOCK_TOKENS, heads, HEAD_SIZE), top_rows, total_rows)


def combine_parts(first, second):
    out_a, top_a, total_a = first
    out_b, top_b, total_b = second
    top = jnp.maximum(top_a, top_b)
    factor_a = jnp.exp(top_a - top)
    factor_b = jnp.exp(top_b - top)
    return (
        out_a * factor_a[..., None] + out_b * factor_b[..., None],
        top,
        total_a * factor_a + total_b * factor_b,
    )


def per_device(queries, keys, values, pattern):
    ctx_count = lax.axis_size("ctx")
    head_count = lax.axis_size("head")
    doc_count = lax.axis_size("doc")
    owner = lax.axis_index("ctx")
    tok_rows = queries.shape[1]
    width = queries.shape[2]
    heads = width // HEAD_SIZE
    key_blocks = keys[0].reshape(NKB_DEV, BLOCK_TOKENS, keys.shape[2])
    value_blocks = values[0].reshape(NKB_DEV, BLOCK_TOKENS, values.shape[2])
    picked, valid = owned_slots(pattern[0], owner)
    whole = lax.all_gather(queries[0], "ctx", axis=0, tiled=True)
    query_block_list = whole.reshape(QB_DEV * ctx_count, BLOCK_TOKENS, width)

    def one_query(items):
        query, chosen, ok = items
        return attend_block(query, key_blocks[chosen], value_blocks[chosen], ok)

    mixed, top, total = lax.map(one_query, (query_block_list, picked, valid))
    mixed = mixed.reshape(QB_DEV * ctx_count * BLOCK_TOKENS, heads, HEAD_SIZE)
    top = top.reshape(QB_DEV * ctx_count * BLOCK_TOKENS, heads)
    total = total.reshape(QB_DEV * ctx_count * BLOCK_TOKENS, heads)
    mixed, top, total = joined((mixed, top, total), "ctx", combine_parts)
    mine_mixed = lax.dynamic_slice_in_dim(mixed, owner * tok_rows, tok_rows, 0)
    mine_total = lax.dynamic_slice_in_dim(total, owner * tok_rows, tok_rows, 0)
    attended = (mine_mixed / mine_total[..., None]).astype(jnp.bfloat16).reshape(tok_rows, width)
    sub = width // ctx_count
    model_width = width * head_count
    span = lax.all_gather(attended, "ctx", axis=0, tiled=True)
    mine_cols = lax.dynamic_slice_in_dim(span, owner * sub, sub, 1)
    full_doc = lax.all_gather(span, "head", axis=1, tiled=True)
    slice_width = model_width // doc_count
    split_cols = full_doc.reshape(tok_rows * ctx_count, doc_count, slice_width)
    column_set = lax.all_to_all(split_cols, "doc", split_axis=1, concat_axis=0, tiled=True).reshape(
        doc_count * tok_rows * ctx_count, slice_width
    )
    product = lax.dot_general(
        lax.all_gather(mine_cols, "doc", axis=0, tiled=True),
        column_set,
        (((0,), (0,)), ((), ())),
        preferred_element_type=jnp.float32,
    )
    return (attended.reshape(1, tok_rows, width), product)


def solution(mesh):
    placed = (
        P("doc", "ctx", "head"),
        P("doc", "ctx", "head"),
        P("doc", "ctx", "head"),
        P("doc", None, None),
    )
    return jax.shard_map(
        per_device,
        mesh=mesh,
        in_specs=placed,
        out_specs=(P("doc", "ctx", "head"), P(("head", "ctx"), "doc")),
        check_vma=False,
    )
```

profile of v0, /device:TPU:29, one launch (start us, length us, event | category | flops | bytes accessed | tf_op | source)
XLA Modules:
  0.0 300.9 jit_solution(6687807084662110579)
XLA Ops:
  9.7 0.8 gather_fusion.3
  10.7 1.5 gather_fusion.2
  12.6 7.6 %all-gather.15.cloned.1.call-done = bf16[1,256,2048]{2,1,0:T(8,128)(2,1)} async-done(((bf16[1,128,2048]{2,1,0:T(8,128)(2,1)}), bf16[1,256,2048]{2,1,0:T(8,128)(2,1)}) %all-gather.15.cloned.1.call-update) | async-done | bytes 1048592 | tf_op jit(solution)/shard_map/all_gather | solution.py:83
  20.2 43.3 %while.2 = (s32[]{:T(128)}, f32[2,128,16,128]{3,2,1,0:T(8,128)}, f32[2,128,16]{1,0,2:T(2,128)S(1)}, f32[2,128,16]{1,0,2:T(2,128)S(1)}, s32[2,12]{1,0:T(2,128)S(1...) while((s32[]{:T(128)}, f32[2,128,16,128]{3,2,1,0:T(8,128)}, ...), condition=%wide.region_4.5_spmd, body=%wide.region_1.4_spmd.sunk | while | flops 1651504128 | bytes 103885744 | solution.py:90
  20.2 2.2 gather_fusion
  22.7 1.1 constant_dynamic-slice_fusion.6
  24.1 2.1 bitcast_reduce_fusion.2
  26.2 3.8 %fusion.40 = f32[2,8,128]{2,1,0:T(8,128)S(1)} fusion(f32[2,1536,128,8]{2,1,3,0:T(8,128)S(1)} %get-tuple-element.193, f32[2,8,128]{2,1,0:T(8,128)S(1)} %get-tuple-element.194, pred[1536]{0:T(1024)(128)(4,1)S(1)} %broadcast_bitcast_fusion.2), kind=kLoop, calls=%fused_computation.9.clone.1 | loop fusion | flops 15726592 | bytes 12600832 | tf_op jit(solution)/shard_map/while/body/eval_jaxpr/reduce_sum | solution.py:46
  30.7 2.2 gather_fusion.1
  33.1 7.1 %fusion.39 = f32[2,128,8,128]{3,1,2,0:T(8,128)S(1)} fusion(f32[2,1536,128,8]{2,1,3,0:T(8,128)} %copy-done, f32[2,8,128]{2,1,0:T(8,128)S(1)} %get-tuple-element.194, pred[1536]{0:T(1024)(128)(4,1)S(1)} %broadcast_bitcast_fusion.2, bf16[1536,2,128,1]{2,1,0,3:T(2,128)(2,1)S(1)} %bitcast.116), kind=kOutput, calls=%fused_computation.11.clone.1 | convolution fusion | flops 821035008 | bytes 14427648 | tf_op jit(solution)/shard_map/while/body/eval_jaxpr/kgqs,skd->qkgd/dot_general | solution.py:47
  40.8 1.0 constant_dynamic-update-slice_fusion.2
  41.9 2.2 gather_fusion
  44.4 1.1 constant_dynamic-slice_fusion.6
  45.7 2.1 bitcast_reduce_fusion.2
  47.8 3.8 %fusion.40 = f32[2,8,128]{2,1,0:T(8,128)S(1)} fusion(f32[2,1536,128,8]{2,1,3,0:T(8,128)S(1)} %get-tuple-element.193, f32[2,8,128]{2,1,0:T(8,128)S(1)} %get-tuple-element.194, pred[1536]{0:T(1024)(128)(4,1)S(1)} %broadcast_bitcast_fusion.2), kind=kLoop, calls=%fused_computation.9.clone.1 | loop fusion | flops 15726592 | bytes 12600832 | tf_op jit(solution)/shard_map/while/body/eval_jaxpr/reduce_sum | solution.py:46
  52.4 2.2 gather_fusion.1
  54.8 7.1 %fusion.39 = f32[2,128,8,128]{3,1,2,0:T(8,128)S(1)} fusion(f32[2,1536,128,8]{2,1,3,0:T(8,128)} %copy-done, f32[2,8,128]{2,1,0:T(8,128)S(1)} %get-tuple-element.194, pred[1536]{0:T(1024)(128)(4,1)S(1)} %broadcast_bitcast_fusion.2, bf16[1536,2,128,1]{2,1,0,3:T(2,128)(2,1)S(1)} %bitcast.116), kind=kOutput, calls=%fused_computation.11.clone.1 | convolution fusion | flops 821035008 | bytes 14427648 | tf_op jit(solution)/shard_map/while/body/eval_jaxpr/kgqs,skd->qkgd/dot_general | solution.py:47
  62.4 1.0 constant_dynamic-update-slice_fusion.2
  63.6 1.8 all_gather.23
  65.7 1.8 all_gather.24
  67.6 10.9 %all-gather.7.cloned.1.call-done = f32[2,256,16,128]{3,2,1,0:T(8,128)} async-done(((f32[1,256,16,128]{3,2,1,0:T(8,128)}), f32[2,256,16,128]{3,2,1,0:T(8,128)}) %all-gather.7.cloned.1.call-update) | async-done | bytes 4194320 | tf_op jit(solution)/shard_map/all_gather | solution.py:18
  78.6 2.5 slice_bitcast_fusion.1
  81.1 1.0 fusion.18
  82.0 1.2 copy.61
  83.4 10.1 %all-gather.9.cloned.1.call-done = bf16[256,2048]{0,1:T(8,128)(2,1)} async-done(((bf16[128,2048]{0,1:T(8,128)(2,1)}), bf16[256,2048]{0,1:T(8,128)(2,1)}) %all-gather.9.cloned.1.call-update) | async-done | bytes 1048592 | tf_op jit(solution)/shard_map/all_gather | solution.py:100
  93.4 54.6 %all-gather.13.cloned.1.call-done = bf16[256,8192]{0,1:T(8,128)(2,1)} async-done(((bf16[256,2048]{0,1:T(8,128)(2,1)}), bf16[256,8192]{0,1:T(8,128)(2,1)}) %all-gather.13.cloned.1.call-update) | async-done | bytes 4194320 | tf_op jit(solution)/shard_map/all_gather | solution.py:102
  148.0 5.1 %all-to-all-start = ((bf16[256,4,2048]{0,2,1:T(8,128)(2,1)}), bf16[256,4,2048]{0,2,1:T(8,128)(2,1)}, u32[]{:S(2)}, u32[]{:S(2)}) async-start(bf16[256,4,2048]{0,2,1:T(8,128)(2,1)} %bitcast.120), calls=%async_computation | async-start | bytes 8388608 | tf_op jit(solution)/shard_map/all_to_all | solution.py:105
  153.3 0.8 constant_dynamic-slice_fusion.3
  154.1 1.0 reshape_reshape.3
  155.1 122.2 %all-to-all-done = bf16[256,4,2048]{0,2,1:T(8,128)(2,1)} async-done(((bf16[256,4,2048]{0,2,1:T(8,128)(2,1)}), bf16[256,4,2048]{0,2,1:T(8,128)(2,1)}, u32[]{:S(2)}, u32[]{:S(2)}) %all-to-all-start) | async-done | bytes 4194336 | tf_op jit(solution)/shard_map/all_to_all | solution.py:105
  277.3 6.3 %copy.62 = bf16[4,256,1,2048]{3,1,0,2:T(8,128)(2,1)} copy(bf16[4,256,1,2048]{1,3,0,2:T(8,128)(2,1)} %bitcast.29) | data formatting | bytes 8388608 | tf_op jit(solution)/shard_map/all_to_all | solution.py:105
  283.6 10.7 %fusion.25 = f32[1024,2048]{1,0:T(8,128)} fusion(bf16[1024,1024]{0,1:T(8,128)(2,1)} %all-gather.11.cloned.1.call-done, bf16[1024,2048]{1,0:T(8,128)(2,1)} %bitcast.121), kind=kOutput, calls=%fused_computation.65 | convolution fusion | flops 4294967296 | bytes 14680064 | tf_op jit(solution)/shard_map/dot_general | solution.py:108
  (65 shorter events, 7.8 us)
Async XLA Ops:
  7.2 13.1 %all-gather.15.cloned.1.call-start = ((), (), s32[]{:S(2)}) async-start(), calls=%async_computation.5 | async-start | bytes 1572864 | tf_op jit(solution)/shard_map/all_gather | solution.py:83
  7.9 70.7 %all-gather.7.cloned.1.call-start = ((), (), s32[]{:S(2)}) async-start(), calls=%async_computation.1 | async-start | bytes 6291456 | tf_op jit(solution)/shard_map/all_gather | solution.py:18
  26.2 4.5 %copy-start = (f32[2,1536,128,8]{2,1,3,0:T(8,128)}, f32[2,1536,128,8]{2,1,3,0:T(8,128)S(1)}, u32[]{:S(2)}) copy-start(f32[2,1536,128,8]{2,1,3,0:T(8,128)S(1)} %get-tuple-element.193) | copy-start | bytes 37748740 | tf_op jit(solution)/shard_map/while
  47.8 4.5 %copy-start = (f32[2,1536,128,8]{2,1,3,0:T(8,128)}, f32[2,1536,128,8]{2,1,3,0:T(8,128)S(1)}, u32[]{:S(2)}) copy-start(f32[2,1536,128,8]{2,1,3,0:T(8,128)S(1)} %get-tuple-element.193) | copy-start | bytes 37748740 | tf_op jit(solution)/shard_map/while
  63.5 29.9 %all-gather.9.cloned.1.call-start = ((), (), s32[]{:S(2)}) async-start(), calls=%async_computation.2 | async-start | bytes 1572864 | tf_op jit(solution)/shard_map/all_gather | solution.py:100
  83.3 64.7 %all-gather.13.cloned.1.call-start = ((), (), s32[]{:S(2)}) async-start(), calls=%async_computation.4 | async-start | bytes 5242880 | tf_op jit(solution)/shard_map/all_gather | solution.py:102
  148.0 5.2 %copy-start.1 = (bf16[256,2048]{0,1:T(8,128)(2,1)S(1)}, bf16[256,2048]{0,1:T(8,128)(2,1)}, u32[]{:S(2)}) copy-start(bf16[256,2048]{0,1:T(8,128)(2,1)} %all-gather.9.cloned.1.call-done) | copy-start | bytes 3145732
  148.0 129.3 %all-to-all-start = ((bf16[256,4,2048]{0,2,1:T(8,128)(2,1)}), bf16[256,4,2048]{0,2,1:T(8,128)(2,1)}, u32[]{:S(2)}, u32[]{:S(2)}) async-start(bf16[256,4,2048]{0,2,1:T(8,128)(2,1)} %bitcast.120), calls=%async_computation | async-start | bytes 8388608 | tf_op jit(solution)/shard_map/all_to_all | solution.py:105
  153.2 130.5 %all-gather.11.cloned.1.call-start = ((), (), s32[]{:S(2)}) async-start(), calls=%async_computation.3 | async-start | bytes 2621440 | tf_op jit(solution)/shard_map/all_gather | solution.py:109
Sparse Core Ops, SparseCore 0:
  9.5 10.6 all-gather.14
  63.6 14.8 all-gather.6
  83.4 9.9 all-gather.8
  95.1 52.8 all-gather.12
  155.8 111.3 all-gather.10
where the time goes:
time: 306 us; the launch traced here: 301 us
  waiting for transfers between devices  206 us (67%)
  local copies, waits for them, and re-layouts  32.6 us (11%)
  matrix products  29.1 us (10%)
  between operations  13.9 us (5%)
  other arithmetic  10 us (3%)
  starting transfers between devices  5.37 us (2%)
  blocking collectives  3.66 us (1%)
    all_to_all x1, waiting for transfers between devices, per_device(): lax.all_to_all(split_cols, 'doc', split_axis=1, concat_axis=0, tiled=True)  122 us
    all_gather x1, waiting for transfers between devices, per_device(): full_doc = lax.all_gather(span, 'head', axis=1, tiled=True)  54.6 us
    dot_general x2, matrix products, attend_block(): jnp.einsum('kgqs,skd->qkgd', weights.astype(jnp.bfloat16), value_row_list...  14.2 us
    all_gather x1, waiting for transfers between devices, joined(): pieces = jax.tree.map(lambda part: lax.all_gather(part, axis), value)  10.9 us
    dot_general x1, matrix products, per_device(): lax.dot_general(lax.all_gather(mine_cols, 'doc', axis=0, tiled=True), col...  10.7 us
    all_gather x1, waiting for transfers between devices, per_device(): span = lax.all_gather(attended, 'ctx', axis=0, tiled=True)  10.1 us
    gather x4, local copies, waits for them, and re-layouts, one_query(): return attend_block(query, key_blocks[chosen], value_blocks[chosen], ok)  8.76 us
    all_gather x1, waiting for transfers between devices, per_device(): whole = lax.all_gather(queries[0], 'ctx', axis=0, tiled=True)  7.59 us
  transfers between devices with their start and end apart: 6, of which 5 were waited for; matrix products, arithmetic and copies ran while one was open for 4% of the time, Pallas kernels for 0%

commit v1 on v0

v1 whole, which is shorter than its diff:
```python
import functools
import math

import jax
import jax.numpy as jnp
from jax import lax
from jax.experimental import pallas as pl
from jax.experimental.pallas import tpu as pltpu
from jax.sharding import PartitionSpec as P

HEAD_SIZE = 128
BLOCK_TOKENS = 128
GROUP = 8
CAP = 12
CHUNKS = 4
MESH = pl.DeviceIdType.MESH


def slot_table(pattern, row, owner, shard_blocks, count):
    entries = pattern.shape[2]
    low = owner * shard_blocks
    seen = jnp.int32(0)
    slots = [jnp.int32(0)] * count
    for j in range(entries):
        value = pattern[0, row, j] - low
        mine = jnp.logical_and(value >= 0, value < shard_blocks)
        for s in range(min(j + 1, count)):
            slots[s] = jnp.where(jnp.logical_and(mine, seen == s), value, slots[s])
        seen = seen + jnp.where(mine, 1, 0).astype(jnp.int32)
    return slots, seen


def pack_kernel(pat, k_ref, v_ref, out_ref, sem):
    c = lax.axis_index("ctx")
    give, _ = slot_table(pat, 1 - c, c, k_ref.shape[0] // BLOCK_TOKENS, CAP)
    copies = []
    for s in range(CAP):
        there = pl.ds(pl.multiple_of(give[s] * BLOCK_TOKENS, BLOCK_TOKENS), BLOCK_TOKENS)
        here = pl.ds(s * BLOCK_TOKENS, BLOCK_TOKENS)
        for n, ref in enumerate((k_ref, v_ref)):
            copies.append(pltpu.make_async_copy(ref.at[there, :], out_ref.at[n, here, :], sem.at[n, s]))
    for copy in copies:
        copy.start()
    for copy in copies:
        copy.wait()


def swap_kernel(x_ref, out_ref, send_sem, recv_sem):
    peer = 1 - lax.axis_index("ctx")
    barrier = pltpu.get_barrier_semaphore()
    pl.semaphore_signal(barrier, inc=1, device_id={"ctx": peer}, device_id_type=MESH)
    pl.semaphore_wait(barrier, 1)
    copy = pltpu.make_async_remote_copy(
        src_ref=x_ref, dst_ref=out_ref, send_sem=send_sem, recv_sem=recv_sem,
        device_id={"ctx": peer}, device_id_type=MESH)
    copy.start()
    copy.wait()


def attend_kernel(pat, q_ref, k_ref, v_ref, far_ref, att_ref, kg, vg, sem):
    c = lax.axis_index("ctx")
    tokens, width = q_ref.shape
    entries = pat.shape[2]
    own, owned = slot_table(pat, c, c, k_ref.shape[0] // BLOCK_TOKENS, CAP)

    def block(ref, at):
        return ref.at[pl.ds(pl.multiple_of(at * BLOCK_TOKENS, BLOCK_TOKENS), BLOCK_TOKENS), :]

    def pair(p, k_src, v_src):
        here = pl.ds(p * BLOCK_TOKENS, BLOCK_TOKENS)
        return (pltpu.make_async_copy(k_src, kg.at[here, :], sem.at[0, p]),
                pltpu.make_async_copy(v_src, vg.at[here, :], sem.at[1, p]))

    for p in range(entries):
        if p < CAP:
            @pl.when(p < owned)
            def _():
                for copy in pair(p, block(k_ref, own[p]), block(v_ref, own[p])):
                    copy.start()

        @pl.when(p >= owned)
        def _():
            slot = jnp.clip(p - owned, 0, CAP - 1)
            for copy in pair(p, block(far_ref.at[0], slot), block(far_ref.at[1], slot)):
                copy.start()
    for p in range(entries):
        for copy in pair(p, block(k_ref, 0), block(v_ref, 0)):
            copy.wait()

    factor = HEAD_SIZE ** (-0.5) * math.log2(math.e)

    def two_heads(t, carry):
        at = pl.multiple_of(t * 2 * HEAD_SIZE, 2 * HEAD_SIZE)
        pair = q_ref[:, pl.ds(at, 2 * HEAD_SIZE)]
        q2 = jnp.concatenate([pair[:, :HEAD_SIZE], pair[:, HEAD_SIZE:]], axis=0)
        lane = pl.ds(pl.multiple_of((t * 2 // GROUP) * HEAD_SIZE, HEAD_SIZE), HEAD_SIZE)
        scores = lax.dot_general(q2, kg[:, lane], (((1,), (1,)), ((), ())),
                                 preferred_element_type=jnp.float32)
        top = jnp.max(scores, axis=-1, keepdims=True)
        weights = jnp.exp2((scores - top) * factor)
        total = jnp.sum(weights, axis=-1, keepdims=True)
        mixed = jnp.dot(weights.astype(jnp.bfloat16), vg[:, lane], preferred_element_type=jnp.float32)
        out = (mixed / total).astype(jnp.bfloat16)
        att_ref[:, pl.ds(at, 2 * HEAD_SIZE)] = jnp.concatenate([out[:tokens], out[tokens:]], axis=1)
        return carry

    lax.fori_loop(0, width // (2 * HEAD_SIZE), two_heads, 0)


def gather_kernel(docs, att_ref, rows_ref, cols_ref, gath, own_sem,
                  z_up, z_down, z_recv, x_send, x_recv, pr_send, pr_recv, pc_send, pc_recv, lr_sem, lc_sem):
    c = lax.axis_index("ctx")
    h = lax.axis_index("head")
    d = lax.axis_index("doc")
    peer = 1 - c
    tokens, width = att_ref.shape
    x_next = h + 1 - 2 * (h % 2)
    y_next = (h + 2) % 4
    take = pltpu.make_async_copy(att_ref, gath.at[d], own_sem)
    take.start()

    barrier = pltpu.get_barrier_semaphore()

    def greet(where):
        pl.semaphore_signal(barrier, inc=1, device_id=where, device_id_type=MESH)

    greet({"ctx": peer})
    greet({"head": x_next})
    greet({"head": y_next})

    @pl.when(d > 0)
    def _():
        greet({"doc": d - 1})

    @pl.when(d < docs - 1)
    def _():
        greet({"doc": d + 1})

    ends = jnp.where(d > 0, 1, 0) + jnp.where(d < docs - 1, 1, 0)
    pl.semaphore_wait(barrier, 3 + ends)
    take.wait()

    piece = tokens // CHUNKS
    half = width // 2
    total_events = docs * CHUNKS
    rx = (h % 2 + d % 2) % 2
    ry = (h // 2 + d // 2) % 2

    def span(k):
        return pl.ds(pl.multiple_of(k * piece, piece), piece)

    def remote(src, dst, send, recv, where):
        return pltpu.make_async_remote_copy(src_ref=src, dst_ref=dst, send_sem=send, recv_sem=recv,
                                            device_id=where, device_id_type=MESH)

    def up(i, k):
        ref = gath.at[i, span(k), :]
        return remote(ref, ref, z_up.at[i, k], z_recv.at[i, k], {"doc": d + 1})

    def down(i, k):
        ref = gath.at[i, span(k), :]
        return remote(ref, ref, z_down.at[i, k], z_recv.at[i, k], {"doc": d - 1})

    def row_copy(i, k):
        cut = pl.ds(pl.multiple_of(peer * half, half), half)
        return remote(gath.at[i, span(k), cut], rows_ref.at[i, c, span(k), :],
                      pr_send.at[i, k], pr_recv.at[i, k], {"ctx": peer})

    def row_local(i, k):
        cut = pl.ds(pl.multiple_of(c * half, half), half)
        return pltpu.make_async_copy(gath.at[i, span(k), cut], rows_ref.at[i, c, span(k), :], lr_sem.at[i, k])

    def col_local(i, k):
        return pltpu.make_async_copy(gath.at[i, span(k), :], cols_ref.at[i, c, span(k), :], lc_sem.at[i, k])

    def col_copy(i, k, src):
        return remote(src.at[span(k), :], cols_ref.at[i, c, span(k), :],
                      pc_send.at[i, k], pc_recv.at[i, k], {"ctx": peer})

    def plane_copy(i, k, src, head):
        return remote(src.at[span(k), :], cols_ref.at[i, c, span(k), :],
                      x_send.at[i, k], x_recv.at[i, k], {"head": head})

    def hop_of(par):
        first = jnp.where(par == 0, rx, ry)
        second = jnp.where(par == 0, ry, rx)
        return first + second * (3 - 2 * first)

    def next_of(par, hop):
        return jnp.where((par + hop) % 2 == 0, x_next, y_next)

    def item(side, s):
        i = d - s if side == 0 else d + s
        there = (i >= 0) if side == 0 else jnp.logical_and(i < docs, s > 0)
        return i, there

    def z_part(e):
        s, k = e // CHUNKS, e % CHUNKS
        for side in range(2):
            i, there = item(side, s)

            @pl.when(jnp.logical_and(there, e < total_events))
            def _():
                @pl.when(s > 0)
                def _():
                    up(i, k).wait_recv()

                @pl.when(jnp.logical_and(i <= d, d < docs - 1))
                def _():
                    up(i, k).start()

                @pl.when(jnp.logical_and(i >= d, d > 0))
                def _():
                    down(i, k).start()

                row_copy(i, k).start()
                row_local(i, k).start()

    def x_part(e):
        par = e % 2
        hop = hop_of(par)
        ee = e - 2 * hop
        inside = jnp.logical_and(ee >= 0, ee < total_events)
        at = jnp.where(inside, ee, 0)
        s, k = at // CHUNKS, at % CHUNKS
        for side in range(2):
            i, there = item(side, s)
            there = jnp.logical_and(there, inside)

            @pl.when(jnp.logical_and(there, hop == 0))
            def _():
                plane_copy(i, k, gath.at[i], next_of(par, hop)).start()
                col_copy(i, k, gath.at[i]).start()
                col_local(i, k).start()

            @pl.when(jnp.logical_and(there, hop > 0))
            def _():
                src = cols_ref.at[i, c]
                plane_copy(i, k, src, x_next).wait_recv()

                @pl.when(hop < 3)
                def _():
                    plane_copy(i, k, src, next_of(par, hop)).start()

                col_copy(i, k, src).start()

    def event(e, carry):
        z_part(e)
        x_part(e)
        return carry

    lax.fori_loop(0, total_events + 6, event, 0)

    def finish(n, carry):
        i, k = n // CHUNKS, n % CHUNKS
        par = k % 2
        hop = hop_of(par)

        @pl.when(jnp.logical_and(i <= d, d < docs - 1))
        def _():
            up(i, k).wait_send()

        @pl.when(jnp.logical_and(i >= d, d > 0))
        def _():
            down(i, k).wait_send()

        row_copy(i, k).wait()
        row_local(i, k).wait()
        col_copy(i, k, cols_ref.at[i, c]).wait()

        @pl.when(hop < 3)
        def _():
            plane_copy(i, k, cols_ref.at[i, c], x_next).wait_send()

        @pl.when(hop == 0)
        def _():
            col_local(i, k).wait()

        return carry

    lax.fori_loop(0, total_events, finish, 0)


def attention(queries, keys, values, pattern):
    wide = keys.shape[1]
    entries = pattern.shape[2]
    bf16 = jnp.bfloat16
    vmem = pl.BlockSpec(memory_space=pltpu.VMEM)
    smem = pl.BlockSpec(memory_space=pltpu.SMEM)
    hbm = pl.BlockSpec(memory_space=pl.ANY)
    packed_shape = jax.ShapeDtypeStruct((2, CAP * BLOCK_TOKENS, wide), bf16)
    packed = pl.pallas_call(
        pack_kernel,
        out_shape=packed_shape,
        in_specs=[smem, hbm, hbm],
        out_specs=vmem,
        scratch_shapes=[pltpu.SemaphoreType.DMA((2, CAP))],
    )(pattern, keys, values)
    far = pl.pallas_call(
        swap_kernel,
        out_shape=packed_shape,
        in_specs=[hbm],
        out_specs=hbm,
        scratch_shapes=[pltpu.SemaphoreType.DMA] * 2,
        compiler_params=pltpu.CompilerParams(collective_id=0, has_side_effects=True),
    )(packed)
    return pl.pallas_call(
        attend_kernel,
        out_shape=jax.ShapeDtypeStruct(queries.shape, bf16),
        in_specs=[smem, vmem, hbm, hbm, hbm],
        out_specs=vmem,
        scratch_shapes=[pltpu.VMEM((entries * BLOCK_TOKENS, wide), bf16)] * 2
        + [pltpu.SemaphoreType.DMA((2, entries))],
    )(pattern, queries, keys, values, far)


def gathered(attended, docs):
    tokens, width = attended.shape
    bf16 = jnp.bfloat16
    vmem = pl.BlockSpec(memory_space=pltpu.VMEM)
    return pl.pallas_call(
        functools.partial(gather_kernel, docs),
        out_shape=[
            jax.ShapeDtypeStruct((docs, 2, tokens, width // 2), bf16),
            jax.ShapeDtypeStruct((docs, 2, tokens, width), bf16),
        ],
        in_specs=[pl.BlockSpec(memory_space=pl.ANY)],
        out_specs=[vmem, vmem],
        scratch_shapes=[pltpu.VMEM((docs, tokens, width), bf16), pltpu.SemaphoreType.DMA]
        + [pltpu.SemaphoreType.DMA((docs, CHUNKS))] * 11,
        compiler_params=pltpu.CompilerParams(collective_id=1, has_side_effects=True),
    )(attended)


def per_device(queries, keys, values, pattern):
    ctx_count = lax.axis_size("ctx")
    head_count = lax.axis_size("head")
    doc_count = lax.axis_size("doc")
    owner = lax.axis_index("ctx")
    tok_rows = queries.shape[1]
    width = queries.shape[2]
    direct = head_count == 4 and doc_count == 4
    attended = attention(queries[0], keys[0], values[0], pattern)
    contract = (((0,), (0,)), ((), ()))
    if direct:
        rows, cols = gathered(attended, doc_count)
        tokens = doc_count * ctx_count * tok_rows
        product = lax.dot_general(
            rows.reshape(tokens, width // ctx_count), cols.reshape(tokens, width), contract,
            preferred_element_type=jnp.float32)
        return (attended[None], product)
    sub = width // ctx_count
    model_width = width * head_count
    span = lax.all_gather(attended, "ctx", axis=0, tiled=True)
    mine_cols = lax.dynamic_slice_in_dim(span, owner * sub, sub, 1)
    full_doc = lax.all_gather(span, "head", axis=1, tiled=True)
    slice_width = model_width // doc_count
    split_cols = full_doc.reshape(tok_rows * ctx_count, doc_count, slice_width)
    column_set = lax.all_to_all(split_cols, "doc", split_axis=1, concat_axis=0, tiled=True).reshape(
        doc_count * tok_rows * ctx_count, slice_width)
    product = lax.dot_general(
        lax.all_gather(mine_cols, "doc", axis=0, tiled=True), column_set, contract,
        preferred_element_type=jnp.float32)
    return (attended[None], product)


def solution(mesh):
    placed = (
        P("doc", "ctx", "head"),
        P("doc", "ctx", "head"),
        P("doc", "ctx", "head"),
        P("doc", None, None),
    )
    return jax.shard_map(
        per_device,
        mesh=mesh,
        in_specs=placed,
        out_specs=(P("doc", "ctx", "head"), P(("head", "ctx"), "doc")),
        check_vma=False,
    )
```

time: 306 us -> 86.4 us (0.28); the launches traced: 301 us -> 86.1 us
  waiting for transfers between devices: 206 us -> 0 us
  Pallas kernels: 0 us -> 74.6 us
  local copies, waits for them, and re-layouts: 32.6 us -> 0 us
  matrix products: 29.1 us -> 10.8 us
  between operations: 13.9 us -> 0.66 us
  other arithmetic: 10 us -> 0 us
  starting transfers between devices: 5.37 us -> 0 us
  blocking collectives: 3.66 us -> 0 us
    all_to_all x1 -> x0, waiting for transfers between devices: 122 us -> none  [per_device(): lax.all_to_all(split_cols, 'doc', split_axis=1, concat_axis=0, tiled=True)]
    all_gather x5 -> x0, waiting for transfers between devices: 83.2 us -> none  [the longest x1 54.6 us: per_device(): full_doc = lax.all_gather(span, 'head', axis=1, tiled=True)]
    pallas_call x0 -> x4, Pallas kernels: none -> 74.6 us  [the longest x1 54.6 us: gathered(): pl.pallas_call(functools.partial(gather_kernel, docs), out_shape=[jax.Sha...]
    dot_general x5 -> x1, matrix products: 29.1 us -> 10.8 us  [per_device(): lax.dot_general(rows.reshape(tokens, width // ctx_count), cols.reshape(to...]
    gather x12 -> x0, local copies, waits for them, and re-layouts: 11.7 us -> none  [the longest x4 8.76 us: one_query(): return attend_block(query, key_blocks[chosen], value_blocks[chosen], ok)]
    reduce_sum x2 -> x0, other arithmetic: 7.55 us -> none  [attend_block(): total = jnp.sum(weights, axis=-1)]
    all_to_all x1 -> x0, local copies, waits for them, and re-layouts: 6.33 us -> none  [per_device(): lax.all_to_all(split_cols, 'doc', split_axis=1, concat_axis=0, tiled=True)]
    all_to_all x1 -> x0, starting transfers between devices: 5.15 us -> none  [per_device(): lax.all_to_all(split_cols, 'doc', split_axis=1, concat_axis=0, tiled=True)]
  transfers between devices with their start and end apart: 6 -> 0, of which waited for: 5 -> 0; matrix products, arithmetic and copies ran while one was open for 4% -> 0% of each run, Pallas kernels for 0% -> 0%
where the time goes in v1:
time: 86.4 us; the launch traced here: 86.1 us
  Pallas kernels  74.6 us (86%)
  matrix products  10.8 us (12%)
    pallas_call x1, Pallas kernels, gathered(): pl.pallas_call(functools.partial(gather_kernel, docs), out_shape=[jax.Sha...  54.6 us
    pallas_call x1, Pallas kernels, attention(): pl.pallas_call(attend_kernel, out_shape=jax.ShapeDtypeStruct(queries.shap...  12.3 us
    dot_general x1, matrix products, per_device(): lax.dot_general(rows.reshape(tokens, width // ctx_count), cols.reshape(to...  10.8 us
    pallas_call x1, Pallas kernels, attention(): pl.pallas_call(swap_kernel, out_shape=packed_shape, in_specs=[hbm], out_s...  4.11 us
    pallas_call x1, Pallas kernels, attention(): pl.pallas_call(pack_kernel, out_shape=packed_shape, in_specs=[smem, hbm,...  3.56 us

profile of v1, /device:TPU:29, one launch (start us, length us, event | category | flops | bytes accessed | tf_op | source)
XLA Modules:
  0.0 86.1 jit_solution(13339178061010365568)
XLA Ops:
  0.6 3.6 %shard_map.59.x_ref = bf16[2,1536,256]{2,1,0:T(8,128)(2,1)} custom-call(s32[1,2,16]{2,1,0:T(2,128)} %pat.3, bf16[4096,256]{1,0:T(8,128)(2,1)} %bitcast.10, bf16[4096,256]{1,0:T(8,128)(2,1)} %bitcast.12), custom_call_target="tpu_custom_call" | custom-call | tf_op jit(solution)/shard_map/pallas_call | solution.py:292
  4.2 4.1 %shard_map.60.far_ref = bf16[2,1536,256]{2,1,0:T(8,128)(2,1)} custom-call(bf16[2,1536,256]{2,1,0:T(8,128)(2,1)} %shard_map.59.x_ref), custom_call_target="tpu_custom_call" | custom-call | tf_op jit(solution)/shard_map/pallas_call | solution.py:299
  8.3 12.3 %shard_map.61.att_ref = bf16[128,2048]{1,0:T(8,128)(2,1)} custom-call(s32[1,2,16]{2,1,0:T(2,128)} %pat.3, bf16[128,2048]{1,0:T(8,128)(2,1)} %bitcast.15, bf16[4096,256]{1,0:T(8,128)(2,1)} %bitcast.11, bf16[4096,256]{1,0:T(8,128)(2,1)} %bitcast.13, bf16[2,1536,256]{2,1,0:T(8,128)(2,1)} %shard_map.60.far_ref), custom_call_target="tpu_custom_call" | custom-call | tf_op jit(solution)/shard_map/pallas_call | solution.py:307
  20.7 54.6 %shard_map.62 = (bf16[4,2,128,1024]{3,2,1,0:T(8,128)(2,1)}, bf16[4,2,128,2048]{3,2,1,0:T(8,128)(2,1)}) custom-call(bf16[128,2048]{1,0:T(8,128)(2,1)} %shard_map.61.att_ref), custom_call_target="tpu_custom_call" | custom-call | tf_op jit(solution)/shard_map/pallas_call | solution.py:321
  75.3 10.8 %convolution_bitcast_fusion = f32[1024,2048]{1,0:T(8,128)} fusion(bf16[4,2,128,1024]{3,2,1,0:T(8,128)(2,1)} %get-tuple-element.4, bf16[4,2,128,2048]{3,2,1,0:T(8,128)(2,1)} %get-tuple-element.5), kind=kOutput, calls=%fused_computation | convolution fusion | flops 4294967296 | bytes 14680064 | tf_op jit(solution)/shard_map/dot_general | solution.py:348

commit v2 on v0

v2 whole, which is shorter than its diff:
```python
import functools
import math

import jax
import jax.numpy as jnp
from jax import lax
from jax.experimental import pallas as pl
from jax.experimental.pallas import tpu as pltpu
from jax.sharding import PartitionSpec as P

HEAD_SIZE = 128
BLOCK_TOKENS = 128
GROUP = 8
WIDE = 2 * HEAD_SIZE
LAG = 4
MESH = pl.DeviceIdType.MESH


def pack_kernel(pat, k_ref, v_ref, own_ref, give_ref, sem):
    c = lax.axis_index("ctx")
    entries = pat.shape[2]
    shard_blocks = k_ref.shape[0] // BLOCK_TOKENS

    def each(action, otherwise):
        for n, (row, out_ref) in enumerate(((1 - c, give_ref), (c, own_ref))):
            for p in range(entries):
                at = pat[0, row, p] - c * shard_blocks
                mine = jnp.logical_and(at >= 0, at < shard_blocks)
                here = pl.ds(p * BLOCK_TOKENS, BLOCK_TOKENS)

                @pl.when(mine)
                def _():
                    there = pl.ds(pl.multiple_of(at * BLOCK_TOKENS, BLOCK_TOKENS), BLOCK_TOKENS)
                    for m, ref in enumerate((k_ref, v_ref)):
                        action(pltpu.make_async_copy(ref.at[there, :], out_ref.at[m, here, :], sem.at[n, m, p]))

                if otherwise:
                    @pl.when(jnp.logical_not(mine))
                    def _():
                        zero = jnp.zeros((BLOCK_TOKENS, k_ref.shape[1]), out_ref.dtype)
                        out_ref[0, here, :] = zero
                        out_ref[1, here, :] = zero

    each(lambda copy: copy.start(), True)
    each(lambda copy: copy.wait(), False)


def main_kernel(docs, gather, q_any, own_any, give_any, att_ref, *refs):
    if gather:
        (rows_ref, cols_ref, q_ref, own, recv, kv, in_sem, kv_send, kv_recv, gath, colbuf,
         z_up, z_down, z_recv, x_send, x_more, x_recv, r_send, r_recv, p_send, p_recv, r_local, c_local) = refs
    else:
        q_ref, own, recv, kv, in_sem, kv_send, kv_recv = refs
    c = lax.axis_index("ctx")
    h = lax.axis_index("head")
    d = lax.axis_index("doc")
    peer = 1 - c
    tokens, width = q_ref.shape
    chunks = width // WIDE
    x_next = h + 1 - 2 * (h % 2)
    y_next = (h + 2) % 4

    take_q = pltpu.make_async_copy(q_any, q_ref, in_sem.at[0])
    take_own = pltpu.make_async_copy(own_any, own, in_sem.at[1])
    take_own.start()
    take_q.start()

    barrier = pltpu.get_barrier_semaphore()

    def greet(where):
        pl.semaphore_signal(barrier, inc=1, device_id=where, device_id_type=MESH)

    greet({"ctx": peer})
    if gather:
        greet({"head": x_next})
        greet({"head": y_next})

        @pl.when(d > 0)
        def _():
            greet({"doc": d - 1})

        @pl.when(d < docs - 1)
        def _():
            greet({"doc": d + 1})

        ends = jnp.where(d > 0, 1, 0) + jnp.where(d < docs - 1, 1, 0)
        pl.semaphore_wait(barrier, 3 + ends)
    else:
        pl.semaphore_wait(barrier, 1)

    def remote(src, dst, send, arrive, where):
        return pltpu.make_async_remote_copy(src_ref=src, dst_ref=dst, send_sem=send, recv_sem=arrive,
                                            device_id=where, device_id_type=MESH)

    swaps = [remote(give_any.at[n], recv.at[n], kv_send.at[n], kv_recv.at[n], {"ctx": peer}) for n in range(2)]
    for swap in swaps:
        swap.start()
    take_q.wait()
    take_own.wait()
    for n, swap in enumerate(swaps):
        swap.wait()
        kv[n] = own[n] + recv[n]

    factor = HEAD_SIZE ** (-0.5) * math.log2(math.e)

    def two_heads(t):
        at = pl.multiple_of(t * WIDE, WIDE)
        pair = q_ref[:, pl.ds(at, WIDE)]
        q2 = jnp.concatenate([pair[:, :HEAD_SIZE], pair[:, HEAD_SIZE:]], axis=0)
        lane = pl.ds(pl.multiple_of((t * 2 // GROUP) * HEAD_SIZE, HEAD_SIZE), HEAD_SIZE)
        scores = lax.dot_general(q2, kv[0, :, lane], (((1,), (1,)), ((), ())),
                                 preferred_element_type=jnp.float32)
        top = jnp.max(scores, axis=-1, keepdims=True)
        weights = jnp.exp2((scores - top) * factor)
        total = jnp.sum(weights, axis=-1, keepdims=True)
        mixed = jnp.dot(weights.astype(jnp.bfloat16), kv[1, :, lane], preferred_element_type=jnp.float32)
        out = (mixed / total).astype(jnp.bfloat16)
        out = jnp.concatenate([out[:tokens], out[tokens:]], axis=1)
        if gather:
            gath[d, t] = out
        att_ref[:, pl.ds(at, WIDE)] = out

    if not gather:
        def plain(t, carry):
            two_heads(t)
            return carry

        lax.fori_loop(0, chunks, plain, 0)
        return

    total_events = docs * chunks
    far_step = docs // 2
    half_chunks = chunks // 2
    rx = (h % 2 + d % 2) % 2
    ry = (h // 2 + d // 2) % 2

    def columns(k):
        return pl.ds(pl.multiple_of(k * WIDE, WIDE), WIDE)

    def up(i, k):
        return remote(gath.at[i, k], gath.at[i, k], z_up.at[i, k], z_recv.at[i, k], {"doc": d + 1})

    def down(i, k):
        return remote(gath.at[i, k], gath.at[i, k], z_down.at[i, k], z_recv.at[i, k], {"doc": d - 1})

    def row_home(i, k):
        return rows_ref.at[i, c, :, columns(k % half_chunks)]

    def row_copy(i, k):
        return remote(gath.at[i, k], row_home(i, k), r_send.at[i, k], r_recv.at[i, k], {"ctx": peer})

    def row_local(i, k):
        return pltpu.make_async_copy(gath.at[i, k], row_home(i, k), r_local.at[i, k])

    def col_local(i, k, src):
        return pltpu.make_async_copy(src.at[i, k], cols_ref.at[i, c, :, columns(k)], c_local.at[i, k])

    def col_copy(i, k, src):
        return remote(src.at[i, k], cols_ref.at[i, c, :, columns(k)],
                      p_send.at[i, k], p_recv.at[i, k], {"ctx": peer})

    def plane_copy(i, k, src, sem, head):
        return remote(src.at[i, k], colbuf.at[i, k], sem.at[i, k], x_recv.at[i, k], {"head": head})

    def place(k):
        even = k % 2 == 0
        return (jnp.where(even, rx, ry), jnp.where(even, ry, rx),
                jnp.where(even, x_next, y_next), jnp.where(even, y_next, x_next))

    def item(side, s):
        i = d - s if side == 0 else d + s
        there = (i >= 0) if side == 0 else jnp.logical_and(i < docs, s > 0)
        return i, there

    def z_part(e):
        s, k = e // chunks, e % chunks
        for side in range(2):
            i, there = item(side, s)

            @pl.when(jnp.logical_and(there, e < total_events))
            def _():
                @pl.when(s > 0)
                def _():
                    up(i, k).wait_recv()

                @pl.when(jnp.logical_and(i <= d, d < docs - 1))
                def _():
                    up(i, k).start()

                @pl.when(jnp.logical_and(i >= d, d > 0))
                def _():
                    down(i, k).start()

                @pl.when(k // half_chunks == c)
                def _():
                    row_local(i, k).start()

                @pl.when(k // half_chunks != c)
                def _():
                    row_copy(i, k).start()

    def x_part(e):
        a, b, first, second = place(e)
        hop = a + b * (3 - 2 * a)
        ee = e - LAG * hop
        inside = jnp.logical_and(ee >= 0, ee < total_events)
        at = jnp.where(inside, ee, 0)
        s, k = at // chunks, at % chunks
        near = s < far_step
        for side in range(2):
            i, there = item(side, s)
            there = jnp.logical_and(there, inside)

            @pl.when(jnp.logical_and(there, hop == 0))
            def _():
                plane_copy(i, k, gath, x_send, first).start()

                @pl.when(s >= far_step)
                def _():
                    plane_copy(i, k, gath, x_more, second).start()

                col_copy(i, k, gath).start()
                col_local(i, k, gath).start()

            @pl.when(jnp.logical_and(there, hop > 0))
            def _():
                plane_copy(i, k, colbuf, x_send, first).wait_recv()

                @pl.when(hop == 1)
                def _():
                    plane_copy(i, k, colbuf, x_send, second).start()

                @pl.when(jnp.logical_and(hop == 2, near))
                def _():
                    plane_copy(i, k, colbuf, x_send, first).start()

                col_copy(i, k, colbuf).start()
                col_local(i, k, colbuf).start()

    def opening(e, carry):
        two_heads(e)
        z_part(e)
        x_part(e)
        return carry

    def event(e, carry):
        z_part(e)
        x_part(e)
        return carry

    lax.fori_loop(0, chunks, opening, 0)
    lax.fori_loop(chunks, total_events + 3 * LAG, event, 0)

    def finish(n, carry):
        i, k = n // chunks, n % chunks
        a, b, first, second = place(k)
        hop = a + b * (3 - 2 * a)
        near = jnp.logical_and(i - d < far_step, d - i < far_step)

        @pl.when(jnp.logical_and(i <= d, d < docs - 1))
        def _():
            up(i, k).wait_send()

        @pl.when(jnp.logical_and(i >= d, d > 0))
        def _():
            down(i, k).wait_send()

        @pl.when(k // half_chunks == c)
        def _():
            row_local(i, k).wait()
            row_copy(i, k).wait_recv()

        @pl.when(k // half_chunks != c)
        def _():
            row_copy(i, k).wait_send()

        col_copy(i, k, colbuf).wait()
        col_local(i, k, colbuf).wait()

        @pl.when(jnp.logical_or(hop < 2, jnp.logical_and(hop == 2, near)))
        def _():
            plane_copy(i, k, colbuf, x_send, first).wait_send()

        @pl.when(jnp.logical_and(hop == 0, jnp.logical_not(near)))
        def _():
            plane_copy(i, k, colbuf, x_more, second).wait_send()

        return carry

    lax.fori_loop(0, total_events, finish, 0)


def fused(queries, keys, values, pattern, docs, gather):
    tokens, width = queries.shape
    wide = keys.shape[1]
    entries = pattern.shape[2]
    bf16 = jnp.bfloat16
    vmem = pl.BlockSpec(memory_space=pltpu.VMEM)
    smem = pl.BlockSpec(memory_space=pltpu.SMEM)
    hbm = pl.BlockSpec(memory_space=pl.ANY)
    pack = (2, entries * BLOCK_TOKENS, wide)
    own, give = pl.pallas_call(
        pack_kernel,
        out_shape=[jax.ShapeDtypeStruct(pack, bf16)] * 2,
        in_specs=[smem, hbm, hbm],
        out_specs=[vmem] * 2,
        scratch_shapes=[pltpu.SemaphoreType.DMA((2, 2, entries))],
    )(pattern, keys, values)
    out_shape = [jax.ShapeDtypeStruct((tokens, width), bf16)]
    scratch = [pltpu.VMEM((tokens, width), bf16)] + [pltpu.VMEM(pack, bf16)] * 3
    scratch += [pltpu.SemaphoreType.DMA((2,))] * 3
    if gather:
        chunks = width // WIDE
        out_shape += [
            jax.ShapeDtypeStruct((docs, 2, tokens, width // 2), bf16),
            jax.ShapeDtypeStruct((docs, 2, tokens, width), bf16),
        ]
        scratch += [pltpu.VMEM((docs, chunks, tokens, WIDE), bf16)] * 2
        scratch += [pltpu.SemaphoreType.DMA((docs, chunks))] * 12
    return pl.pallas_call(
        functools.partial(main_kernel, docs, gather),
        out_shape=out_shape,
        in_specs=[hbm] * 3,
        out_specs=[vmem] + [hbm] * (len(out_shape) - 1),
        scratch_shapes=scratch,
        compiler_params=pltpu.CompilerParams(collective_id=0, has_side_effects=True),
    )(queries, own, give)


def per_device(queries, keys, values, pattern):
    ctx_count = lax.axis_size("ctx")
    head_count = lax.axis_size("head")
    doc_count = lax.axis_size("doc")
    owner = lax.axis_index("ctx")
    tok_rows = queries.shape[1]
    width = queries.shape[2]
    direct = head_count == 4 and doc_count == 4
    made = fused(queries[0], keys[0], values[0], pattern, doc_count, direct)
    contract = (((0,), (0,)), ((), ()))
    if direct:
        attended, rows, cols = made
        tokens = doc_count * ctx_count * tok_rows
        product = lax.dot_general(
            rows.reshape(tokens, width // ctx_count), cols.reshape(tokens, width), contract,
            preferred_element_type=jnp.float32)
        return (attended[None], product)
    attended = made[0]
    sub = width // ctx_count
    model_width = width * head_count
    span = lax.all_gather(attended, "ctx", axis=0, tiled=True)
    mine_cols = lax.dynamic_slice_in_dim(span, owner * sub, sub, 1)
    full_doc = lax.all_gather(span, "head", axis=1, tiled=True)
    slice_width = model_width // doc_count
    split_cols = full_doc.reshape(tok_rows * ctx_count, doc_count, slice_width)
    column_set = lax.all_to_all(split_cols, "doc", split_axis=1, concat_axis=0, tiled=True).reshape(
        doc_count * tok_rows * ctx_count, slice_width)
    product = lax.dot_general(
        lax.all_gather(mine_cols, "doc", axis=0, tiled=True), column_set, contract,
        preferred_element_type=jnp.float32)
    return (attended[None], product)


def solution(mesh):
    placed = (
        P("doc", "ctx", "head"),
        P("doc", "ctx", "head"),
        P("doc", "ctx", "head"),
        P("doc", None, None),
    )
    return jax.shard_map(
        per_device,
        mesh=mesh,
        in_specs=placed,
        out_specs=(P("doc", "ctx", "head"), P(("head", "ctx"), "doc")),
        check_vma=False,
    )
```

time: 306 us -> 74.9 us (0.24)
  the two profiles are of different devices: /device:TPU:29 before, /device:TPU:25 now
where the time goes in v2:
time: 74.9 us; the launch traced here: 74.7 us
  Pallas kernels  62.4 us (83%)
  matrix products  10.8 us (14%)
  local copies, waits for them, and re-layouts  0.8 us (1%)
    pallas_call x1, Pallas kernels, fused(): pl.pallas_call(functools.partial(main_kernel, docs, gather), out_shape=ou...  57.5 us
    dot_general x1, matrix products, per_device(): lax.dot_general(rows.reshape(tokens, width // ctx_count), cols.reshape(to...  10.8 us
    pallas_call x1, Pallas kernels, fused(): pl.pallas_call(pack_kernel, out_shape=[jax.ShapeDtypeStruct(pack, bf16)]...  4.88 us

profile of v2, /device:TPU:25, one launch (start us, length us, event | category | flops | bytes accessed | tf_op | source)
XLA Modules:
  0.0 74.7 jit_solution(171699309801570781)
XLA Ops:
  0.6 4.9 %shard_map.59 = (bf16[2,2048,256]{2,1,0:T(8,128)(2,1)}, bf16[2,2048,256]{2,1,0:T(8,128)(2,1)}) custom-call(s32[1,2,16]{2,1,0:T(2,128)} %pat.1, bf16[4096,256]{1,0:T(8,128)(2,1)} %bitcast.10, bf16[4096,256]{1,0:T(8,128)(2,1)} %bitcast.11), custom_call_target="tpu_custom_call" | custom-call | tf_op jit(solution)/shard_map/pallas_call | solution.py:302
  5.5 57.5 %shard_map.60 = (bf16[128,2048]{1,0:T(8,128)(2,1)}, bf16[4,2,128,1024]{3,2,1,0:T(8,128)(2,1)}, bf16[4,2,128,2048]{3,2,1,0:T(8,128)(2,1)}) custom-call(bf16[128,2048]{1,0:T(8,128)(2,1)} %bitcast.12, bf16[2,2048,256]{2,1,0:T(8,128)(2,1)} %get-tuple-element.7.own_any, bf16[2,2048,256]{2,1,0:T(8,128)(2,1)} %get-tuple-element.8.give_any), custom_call_target="tpu_custom_call" | custom-call | tf_op jit(solution)/shard_map/pallas_call | solution.py:320
  63.0 0.0 copy-start
  63.1 10.8 %convolution_bitcast_fusion = f32[1024,2048]{1,0:T(8,128)} fusion(bf16[4,2,128,1024]{3,2,1,0:T(8,128)(2,1)} %get-tuple-element.10, bf16[4,2,128,2048]{3,2,1,0:T(8,128)(2,1)} %get-tuple-element.11), kind=kOutput, calls=%fused_computation | convolution fusion | flops 4294967296 | bytes 14680064 | tf_op jit(solution)/shard_map/dot_general | solution.py:343
  73.9 0.0 copy-done
  73.9 0.8 %copy.10 = bf16[1,128,2048]{2,1,0:T(8,128)(2,1)} copy(bf16[1,128,2048]{2,1,0:T(8,128)(2,1)S(1)} %bitcast.13) | data formatting | bytes 1048576
Async XLA Ops:
  63.0 10.9 %copy-start = (bf16[128,2048]{1,0:T(8,128)(2,1)S(1)}, bf16[128,2048]{1,0:T(8,128)(2,1)}, u32[]{:S(2)}) copy-start(bf16[128,2048]{1,0:T(8,128)(2,1)} %get-tuple-element.9) | copy-start | bytes 1572868
